TPU v7x, 32 devices: a whole 2x2x4 slice. The times are simulated.
32 devices in a mesh: dp: 2 (over x), fsdp: 4 (over y, core), tensor: 4 (over z).
Axes of the slice: x: 2, y: 2, z: 4, core: 2. Of those that a mesh axis runs over, the one named last changes fastest.
Arguments:
- hidden: bfloat16 [4096, 2048], P(('dp', 'fsdp'), 'tensor'), may hold values from -8 to 8
- norm_gain: bfloat16 [2048], P('tensor'), may hold values from 0.099609375 to 1.8984375
- head_weight: bfloat16 [2048, 32128], P('fsdp', 'tensor'), may hold values from -1 to 1
- token_ids: int32 [8, 512], P(('dp', 'fsdp')), may hold values from 0 to 32127
- lengths: int32 [8], P(('dp', 'fsdp')), may hold values from 128 to 512
- old_logp: float32 [8, 512], P(('dp', 'fsdp')), may hold values from -12.5 to -9.5
- advantages: float32 [8, 512], P(('dp', 'fsdp')), may hold values from -4 to 4
- rollout_logp: float32 [8, 512], P(('dp', 'fsdp'), 'tensor'), may hold values from -16 to -1
- rollout_row: int32 [8], P(('dp', 'fsdp')), may hold values from 0 to 7, each once
Outputs:
- new_logp: float32 [8, 512], P(('dp', 'fsdp'))
- token_loss: float32 [8, 512], P(('dp', 'fsdp'))
- summary: float32 [3], replicated
Inputs may be any that keep to these rules, and one draw needn't show every extreme that they name: `rollout_row`: every row 0 to 7 is named once.
All inputs are finite; a program needn't handle non-finite values.
Results may differ from a plain program's by a relative error of at most 0.0005.
The roundings to bfloat16 on the way count: a program that leaves them out, or rounds other values in their place, can miss the bound.
Values may be sent and summed in bfloat16 or wider, within the bound.
A program may use at most 128 MiB of HBM per device.

v0:
```python
import functools

import jax
import jax.numpy as jnp
from jax import lax
from jax.experimental import pallas as pl
from jax.experimental.pallas import tpu as pltpu
from jax.sharding import PartitionSpec as P

MESH = pl.DeviceIdType.MESH
clip_eps = 0.2
kl_coef = 0.2
log_limit = 10.0
norm_eps = 1e-06
LANES = 128
LOW = -1e30


def token_terms(new_logp, old_logp, advantages, ref_logp, live_mask, prob_square):
    shift = new_logp - old_logp
    prob_ratio = jnp.exp(jnp.clip(shift, -log_limit, log_limit))
    clipped = jnp.clip(prob_ratio, 1.0 - clip_eps, 1.0 + clip_eps)
    plain_term = prob_ratio * advantages
    bounded_term = clipped * advantages
    surrogate = jnp.minimum(plain_term, bounded_term)
    ref_gap = ref_logp - new_logp
    gap_clip = jnp.clip(ref_gap, -log_limit, log_limit)
    gap_exp = jnp.exp(gap_clip)
    kl_term = gap_exp - gap_clip - 1.0
    token_loss = live_mask * (kl_coef * kl_term - surrogate)
    gap_part = jnp.where(jnp.abs(ref_gap) < log_limit, kl_coef * (1.0 - gap_exp), 0.0)
    active = (plain_term <= bounded_term) & (jnp.abs(shift) < log_limit)
    grad_coef = live_mask * (gap_part - jnp.where(active, plain_term, 0.0))
    grad_square = grad_coef * grad_coef * (prob_square - 2.0 * jnp.exp(new_logp) + 1.0)
    return (token_loss, live_mask * kl_term, grad_square)


class Config:
    def __init__(self, mesh, tok, dz, kr, vt):
        self.dp, self.fs, self.tz = (mesh.shape[a] for a in ("dp", "fsdp", "tensor"))
        self.groups = self.fs // 2
        self.tok, self.dz, self.kr, self.vt = tok, dz, kr, vt
        self.dim = dz * self.tz
        tiles = -(-vt // LANES)
        self.half_tiles = -(-tiles // (self.groups * self.dp))
        self.half_cols = self.half_tiles * LANES
        self.block_cols = self.half_cols * self.dp
        self.pad_cols = self.block_cols * self.groups
        self.steps = 8
        self.rows = tok // self.steps
        self.chunk = 256 if self.half_cols % 256 == 0 else LANES
        self.wsteps = self.half_cols // self.chunk
        self.pairs = self.steps // 2
        self.pair_rows = 2 * self.rows
        self.resp = self.dp * self.fs


def kernel(
    c,
    hid, gain_in, w_any, id_in, roll_in, old_in, adv_in, len_in, row_in,
    out,
    pack_in, ids_in,
    x_buf, n_buf, w_own, w_full, packs, ids_all, rel, m_buf, l_buf, q_buf, p_buf,
    row_buf, roll, s_out, s_in, t_out, t_in,
    load_sem, x_sem, own_sem, tok_recv, y_send, right_send, left_send,
    wy_send, wy_recv, wx_send, wx_recv, core_send, core_recv,
    ids_send, ids_recv, pack_send, pack_recv, roll_send, roll_recv,
    st_send, st_recv, tot_send, tot_recv,
):
    G, Z, DP, F = c.groups, c.tz, c.dp, c.fs
    x = lax.axis_index("dp")
    f = lax.axis_index("fsdp")
    z = lax.axis_index("tensor")
    g, core = f // 2, f % 2
    partner = (x, g * 2 + (1 - core), z)
    me_resp = x * F + f
    pending = []

    def dev_g(gi):
        return (x, gi * 2 + core, z)

    def dev_x(xi):
        return (xi, f, z)

    def dev_z(zi):
        return (x, f, zi)

    def group(d):
        return lax.rem(g + d, G)

    def remote(src, dst, ss, rs, dev):
        return pltpu.make_async_remote_copy(
            src_ref=src, dst_ref=dst, send_sem=ss, recv_sem=rs, device_id=dev, device_id_type=MESH
        )

    def send(src, dst, ss, rs, dev, cond=None):
        copy = remote(src, dst, ss, rs, dev)
        if cond is None:
            copy.start()
        else:
            pl.when(cond)(copy.start)
        pending.append((cond, copy))

    def arrive(dst, rs, cond=None):
        copy = remote(dst, dst, rs, rs, partner)
        if cond is None:
            copy.wait_recv()
        else:
            pl.when(cond)(copy.wait_recv)

    load = pltpu.make_async_copy(w_any, w_own.at[pl.ds(0, c.vt), :], load_sem)
    load.start()
    zcols = pl.ds(pl.multiple_of(z * c.dz, c.dz), c.dz)
    own_x = pltpu.make_async_copy(hid, x_buf.at[g, :, zcols], x_sem)
    own_x.start()
    if c.vt < c.pad_cols:
        w_own[c.vt :, :] = jnp.zeros((c.pad_cols - c.vt, c.kr), w_own.dtype)
    part = roll_in.shape[1]
    pack_in[:, : c.dz] = jnp.broadcast_to(gain_in[...].astype(jnp.float32), (8, c.dz))
    pack_in[:, c.dz :] = jnp.zeros((8, c.tok), jnp.float32)
    for zi in range(Z):
        @pl.when(z == zi)
        def _(zi=zi):
            pack_in[:, c.dz + zi * part : c.dz + (zi + 1) * part] = jnp.broadcast_to(roll_in[...], (8, part))
    ids_in[...] = jnp.broadcast_to(id_in[...].astype(jnp.float32), (8, c.tok))

    barrier = pltpu.get_barrier_semaphore()
    count = 0
    for dg in range(G):
        for s in range(Z):
            if dg or s:
                pl.semaphore_signal(
                    barrier, inc=1,
                    device_id=(x, group(dg) * 2 + core, lax.rem(z + s, Z)), device_id_type=MESH,
                )
                count += 1
    for dx in range(DP):
        for df in range(F):
            if dx or df % 2:
                pl.semaphore_signal(
                    barrier, inc=1,
                    device_id=(lax.rem(x + dx, DP), lax.rem(f + df, F), z), device_id_type=MESH,
                )
                count += 1
    pl.semaphore_wait(barrier, count)

    def piece(gi, q, zi):
        return x_buf.at[
            gi, pl.ds(q * c.rows, c.rows), pl.ds(pl.multiple_of(zi * c.dz, c.dz), c.dz)
        ]

    def hid_piece(q):
        return hid.at[pl.ds(q * c.rows, c.rows), :]

    def w_block(fi, h, j):
        return w_full.at[
            pl.ds(pl.multiple_of(h * c.half_cols + j * c.chunk, c.chunk), c.chunk),
            pl.ds(pl.multiple_of(fi * c.kr, c.kr), c.kr),
        ]

    def own_block(gi, h, j):
        start = gi * c.block_cols + h * c.half_cols + j * c.chunk
        return w_own.at[pl.ds(pl.multiple_of(start, c.chunk), c.chunk), :]

    def y_tokens(q):
        for d in range(1, G):
            send(hid_piece(q), piece(g, q, z), y_send.at[d, q], tok_recv.at[g, q, z], dev_g(group(d)))

    def y_weights(j):
        for d in range(1, G):
            gi = group(d)
            send(own_block(gi, x, j), w_block(f, x, j), wy_send.at[d, j], wy_recv.at[g, j], dev_g(gi))

    def z_move(q, s):
        right_ok = z - s >= 0
        left_ok = z + s < Z
        zr = jnp.maximum(z - s, 0)
        zl = jnp.minimum(z + s, Z - 1)
        for d in range(G):
            gi = group(d)
            if s == 0:
                if d:
                    arrive(piece(gi, q, z), tok_recv.at[gi, q, z])
                src_r = src_l = hid_piece(q) if d == 0 else piece(gi, q, z)
            else:
                arrive(piece(gi, q, zr), tok_recv.at[gi, q, zr], right_ok)
                arrive(piece(gi, q, zl), tok_recv.at[gi, q, zl], left_ok)
                src_r, src_l = piece(gi, q, zr), piece(gi, q, zl)
            if s < Z - 1:
                send(src_r, piece(gi, q, zr), right_send.at[gi, q, zr], tok_recv.at[gi, q, zr],
                     dev_z(jnp.minimum(z + 1, Z - 1)), right_ok & (z + 1 < Z))
                send(src_l, piece(gi, q, zl), left_send.at[gi, q, zl], tok_recv.at[gi, q, zl],
                     dev_z(jnp.maximum(z - 1, 0)), left_ok & (z >= 1))

    def core_pass(src, fi, h, j):
        gi = fi // 2
        send(src, w_block(fi, h, j), core_send.at[gi, h, j], core_recv.at[gi, h, j], partner)

    for d in range(1, G):
        send(ids_in, ids_all.at[g], ids_send.at[d], ids_recv.at[g], dev_g(group(d)))
    for s in range(1, Z):
        send(pack_in, packs.at[z], pack_send.at[s], pack_recv.at[z], dev_z(lax.rem(z + s, Z)))
    y_tokens(0)

    m_buf[...] = jnp.full(m_buf.shape, LOW, jnp.float32)
    for ref in (l_buf, q_buf, p_buf):
        ref[...] = jnp.zeros(ref.shape, jnp.float32)
    packs[z] = pack_in[...]
    ids_all[g] = ids_in[...]
    load.wait()
    y_weights(0)
    own_copies = []
    for h in range(DP):
        start = pl.multiple_of(g * c.block_cols + h * c.half_cols, LANES)
        copy = pltpu.make_async_copy(
            w_own.at[pl.ds(start, c.half_cols), :],
            w_full.at[pl.ds(h * c.half_cols, c.half_cols), pl.ds(pl.multiple_of(f * c.kr, c.kr), c.kr)],
            own_sem.at[h],
        )
        copy.start()
        own_copies.append(copy)

    def normalize(q):
        rows = pl.ds(q * c.rows, c.rows)
        for gi in range(G):
            values = x_buf[gi, rows, :].astype(jnp.float32)
            inv = lax.rsqrt(jnp.sum(values * values, axis=1, keepdims=True) / c.dim + norm_eps)
            for zi in range(Z):
                gain = packs[zi, 0:1, 0:c.dz]
                part = values[:, zi * c.dz : (zi + 1) * c.dz]
                n_buf[gi, rows, zi * c.dz : (zi + 1) * c.dz] = (part * inv * gain).astype(jnp.bfloat16)

    def unit(p, start, size):
        rows = pl.ds(pl.multiple_of(p * c.pair_rows, c.pair_rows), c.pair_rows)
        width = G * c.pair_rows
        for h in range(DP):
            off = h * c.half_cols + start
            cols = pl.ds(pl.multiple_of(off, c.chunk), size)
            tokens = jnp.concatenate([n_buf[gi, rows, :] for gi in range(G)], axis=0)
            logits = lax.dot_general(
                w_full[cols, :], tokens, (((1,), (1,)), ((), ())), preferred_element_type=jnp.float32
            ).reshape(size // 8, 8, width)
            valid = c.vt - g * c.block_cols - off
            place = rel[p] - off
            index = lax.broadcasted_iota(jnp.int32, (size // 8, 8, 1), 0) * 8 + lax.broadcasted_iota(
                jnp.int32, (size // 8, 8, 1), 1
            )
            p_buf[p] = p_buf[p] + jnp.sum(jnp.where(index == place[None], logits, 0.0), axis=0)
            logits = jnp.where(index < valid, logits, LOW)
            before = m_buf[p]
            top = jnp.maximum(before, jnp.max(logits, axis=0))
            scale = jnp.exp(before - top)
            e = jnp.exp(logits - top[None])
            m_buf[p] = top
            l_buf[p] = l_buf[p] * scale + jnp.sum(e, axis=0)
            q_buf[p] = q_buf[p] * (scale * scale) + jnp.sum(e * e, axis=0)

    for i in range(c.steps + Z - 1):
        if i + 1 < c.steps:
            y_tokens(i + 1)
        if i + 1 < c.wsteps:
            y_weights(i + 1)
        if i < c.wsteps:
            for h in range(DP):
                core_pass(own_block(g, h, i), f, h, i)
        if i < c.steps:
            z_move(i, 0)
        if 0 <= i - 1 < c.wsteps:
            j = i - 1
            for d in range(1, G):
                gi = group(d)
                fi = gi * 2 + core
                arrive(w_block(fi, x, j), wy_recv.at[gi, j])
                for dx in range(1, DP):
                    xi = lax.rem(x + dx, DP)
                    send(w_block(fi, x, j), w_block(fi, x, j), wx_send.at[gi, dx, j],
                         wx_recv.at[gi, x, j], dev_x(xi))
                core_pass(w_block(fi, x, j), fi, x, j)
        for s in range(1, Z - 1):
            if 0 <= i - s < c.steps:
                z_move(i - s, s)
        if 0 <= i - 2 < c.wsteps:
            j = i - 2
            for d in range(1, G):
                gi = group(d)
                fi = gi * 2 + core
                for dx in range(1, DP):
                    xi = lax.rem(x + dx, DP)
                    arrive(w_block(fi, xi, j), wx_recv.at[gi, xi, j])
                    core_pass(w_block(fi, xi, j), fi, xi, j)
        if i == 1:
            for s in range(1, Z):
                zi = lax.rem(z + s, Z)
                arrive(packs.at[zi], pack_recv.at[zi])
            row_buf[...] = sum(packs[zi, :, c.dz :] for zi in range(Z))
            for d in range(1, G):
                arrive(ids_all.at[group(d)], ids_recv.at[group(d)])
            base = z * c.vt + g * c.block_cols
            for p in range(c.pairs):
                for gi in range(G):
                    ids = ids_all[gi, :, p * c.pair_rows : (p + 1) * c.pair_rows]
                    rel[p, :, gi * c.pair_rows : (gi + 1) * c.pair_rows] = ids.astype(jnp.int32) - base
            own_x.wait()
            for copy in own_copies:
                copy.wait()
        if i == 2:
            for dx in range(DP):
                for df in range(F):
                    if dx or df:
                        xi, fi = lax.rem(x + dx, DP), lax.rem(f + df, F)
                        send(row_buf, roll.at[me_resp], roll_send.at[dx, df], roll_recv.at[me_resp],
                             (xi, fi, z))
        q = i - (Z - 1)
        if q >= 0:
            if q < c.wsteps:
                for gi in range(G):
                    for h in range(DP):
                        arrive(w_block(gi * 2 + 1 - core, h, q), core_recv.at[gi, h, q])
                p = q // 2
                if q % 2 or q == c.wsteps - 1:
                    first = q - q % 2
                    if p:
                        pl.loop(0, p)(lambda pp, q=q, first=first: unit(pp, first * c.chunk, (q + 1 - first) * c.chunk))
            z_move(q, Z - 1)
            normalize(q)
            if q % 2:
                ready = min(q + 1, c.wsteps)
                span = min(2, ready)
                pl.loop(0, ready // span)(lambda jj, q=q, span=span: unit(q // 2, jj * (span * c.chunk), span * c.chunk))

    s_out[...] = jnp.zeros(s_out.shape, jnp.float32)
    for p in range(c.pairs):
        m_p = m_buf[p]
        top = jnp.max(m_p, axis=0, keepdims=True)
        scale = jnp.exp(m_p - top)
        total = jnp.sum(l_buf[p] * scale, axis=0, keepdims=True)
        square = jnp.sum(q_buf[p] * (scale * scale), axis=0, keepdims=True)
        picked = jnp.sum(p_buf[p], axis=0, keepdims=True)
        for gi in range(G):
            here = slice(gi * c.pair_rows, (gi + 1) * c.pair_rows)
            there = slice(p * c.pair_rows, (p + 1) * c.pair_rows)
            for k, value in enumerate((top, total, square, picked)):
                s_out[gi, k : k + 1, there] = value[:, here]
    for s in range(Z - 1, -1, -1):
        for d in range(G):
            if s or d:
                gi, zi = group(d), lax.rem(z + s, Z)
                send(s_out.at[gi], s_in.at[g, z], st_send.at[d, s], st_recv.at[g, z],
                     (x, gi * 2 + core, zi))
    s_in[g, z] = s_out[g]

    roll[me_resp] = row_buf[...]
    for dx in range(DP):
        for df in range(F):
            if dx or df:
                r = lax.rem(x + dx, DP) * F + lax.rem(f + df, F)
                arrive(roll.at[r], roll_recv.at[r])
    ref = jnp.zeros((1, c.tok), jnp.float32)
    for r in range(c.resp):
        ref = ref + jnp.where(row_in[0] == r, roll[r, 0:1, :], 0.0)
    position = lax.broadcasted_iota(jnp.int32, (1, c.tok), 1)
    live = jnp.where(position < len_in[0], 1.0, 0.0)

    for s in range(Z):
        for d in range(G):
            if s or d:
                gi, zi = group(d), lax.rem(z + s, Z)
                arrive(s_in.at[gi, zi], st_recv.at[gi, zi])
    every = [(gi, zi) for gi in range(G) for zi in range(Z)]
    top = s_in[0, 0, 0:1, :]
    for gi, zi in every[1:]:
        top = jnp.maximum(top, s_in[gi, zi, 0:1, :])
    total = square = picked = jnp.zeros((1, c.tok), jnp.float32)
    for gi, zi in every:
        scale = jnp.exp(s_in[gi, zi, 0:1, :] - top)
        total = total + s_in[gi, zi, 1:2, :] * scale
        square = square + s_in[gi, zi, 2:3, :] * (scale * scale)
        picked = picked + s_in[gi, zi, 3:4, :]
    new_logp = picked - top - jnp.log(total)
    prob_square = square / (total * total)
    token_loss, kl_part, grad_part = token_terms(
        new_logp, old_in[...], adv_in[...], ref, live, prob_square
    )
    sums = [jnp.sum(v, axis=1, keepdims=True) for v in (live, token_loss, kl_part, grad_part)]
    t_out[...] = jnp.concatenate(
        [jnp.broadcast_to(v, (1, LANES)) for v in sums] + [jnp.zeros((4, LANES), jnp.float32)], axis=0
    )
    for dx in range(DP):
        for df in range(F):
            if dx or df:
                xi, fi = lax.rem(x + dx, DP), lax.rem(f + df, F)
                send(t_out, t_in.at[me_resp], tot_send.at[dx, df], tot_recv.at[me_resp], (xi, fi, z))
    t_in[me_resp] = t_out[...]
    out[0:1, :] = new_logp
    out[1:2, :] = token_loss
    for dx in range(DP):
        for df in range(F):
            if dx or df:
                r = lax.rem(x + dx, DP) * F + lax.rem(f + df, F)
                arrive(t_in.at[r], tot_recv.at[r])
    totals = sum(t_in[r] for r in range(c.resp))
    count = totals[0:1]
    for k, value in enumerate((totals[1:2] / count, totals[2:3] / count, jnp.sqrt(totals[3:4] / count))):
        out[2 + k : 3 + k, :] = jnp.broadcast_to(value[:, 0:1], (1, c.tok))
    out[5:8, :] = jnp.zeros((3, c.tok), jnp.float32)
    for cond, copy in pending:
        if cond is None:
            copy.wait_send()
        else:
            pl.when(cond)(copy.wait_send)


def shards(c_of, hidden, norm_gain, head_weight, token_ids, lengths, old_logp, advantages, rollout_logp, rollout_row):
    c = c_of(hidden.shape[0], hidden.shape[1], head_weight.shape[0], head_weight.shape[1])
    G, Z, DP, F = c.groups, c.tz, c.dp, c.fs
    vmem = pl.BlockSpec(memory_space=pltpu.VMEM)
    smem = pl.BlockSpec(memory_space=pltpu.SMEM)
    hbm = pl.BlockSpec(memory_space=pl.ANY)
    dma = lambda *shape: pltpu.SemaphoreType.DMA(shape)
    f32 = jnp.float32
    lanes = lambda dtype: pltpu.VMEM((c.pairs, 8, G * c.pair_rows), dtype)
    Q, J = c.steps, c.wsteps
    out = pl.pallas_call(
        functools.partial(kernel, c),
        out_shape=jax.ShapeDtypeStruct((8, c.tok), f32),
        in_specs=[vmem, vmem, hbm, vmem, vmem, vmem, vmem, smem, smem],
        out_specs=vmem,
        scratch_shapes=[
            pltpu.VMEM((8, c.dz + c.tok), f32),
            pltpu.VMEM((8, c.tok), f32),
            pltpu.VMEM((G, c.tok, c.dim), jnp.bfloat16),
            pltpu.VMEM((G, c.tok, c.dim), jnp.bfloat16),
            pltpu.VMEM((c.pad_cols, c.kr), jnp.bfloat16),
            pltpu.VMEM((c.block_cols, c.dim), jnp.bfloat16),
            pltpu.VMEM((Z, 8, c.dz + c.tok), f32),
            pltpu.VMEM((G, 8, c.tok), f32),
            lanes(jnp.int32), lanes(f32), lanes(f32), lanes(f32), lanes(f32),
            pltpu.VMEM((8, c.tok), f32),
            pltpu.VMEM((c.resp, 8, c.tok), f32),
            pltpu.VMEM((G, 8, c.tok), f32),
            pltpu.VMEM((G, Z, 8, c.tok), f32),
            pltpu.VMEM((8, LANES), f32),
            pltpu.VMEM((c.resp, 8, LANES), f32),
            pltpu.SemaphoreType.DMA, pltpu.SemaphoreType.DMA, dma(DP), dma(G, Q, Z), dma(G, Q), dma(G, Q, Z), dma(G, Q, Z),
            dma(G, J), dma(G, J), dma(G, DP, J), dma(G, DP, J), dma(G, DP, J), dma(G, DP, J),
            dma(G), dma(G), dma(Z), dma(Z), dma(DP, F), dma(c.resp),
            dma(G, Z), dma(G, Z), dma(DP, F), dma(c.resp),
        ],
        compiler_params=pltpu.CompilerParams(
            collective_id=0, has_side_effects=True, vmem_limit_bytes=64 * 1024 * 1024 - 65536
        ),
    )(hidden, norm_gain[None, :], head_weight.T, token_ids, rollout_logp, old_logp, advantages, lengths, rollout_row)
    return (out[0:1], out[1:2], out[2:5, 0])


def solution(mesh):
    rows = ("dp", "fsdp")
    in_specs = (
        P(rows, "tensor"), P("tensor"), P("fsdp", "tensor"), P(rows, None), P(rows),
        P(rows, None), P(rows, None), P(rows, "tensor"), P(rows),
    )
    out_specs = (P(rows, None), P(rows, None), P())
    return jax.shard_map(
        functools.partial(shards, functools.partial(Config, mesh)),
        mesh=mesh, in_specs=in_specs, out_specs=out_specs, check_vma=False,
    )
```

profile of v0, /device:TPU:0, one launch (start us, length us, event | category | flops | bytes accessed | tf_op | source)
XLA Modules:
  0.0 112.9 jit_solution(7380379604846909821)
XLA Ops:
  0.6 1.3 %broadcast_in_dim.3.gain_in = bf16[1,512]{1,0:T(2,128)(2,1)} reshape(bf16[512]{0:T(512)(128)(2,1)} %param.10) | data formatting | bytes 2048 | tf_op jit(solution)/shard_map/broadcast_in_dim | solution.py:452
  3.2 107.0 %shard_map.112 = f32[8,512]{1,0:T(8,128)} custom-call(bf16[512,512]{1,0:T(8,128)(2,1)} %hid.1, bf16[1,512]{1,0:T(2,128)(2,1)} %broadcast_in_dim.3.gain_in, bf16[8032,512]{1,0:T(8,128)(2,1)} %bitcast.1, s32[1,512]{1,0:T(1,128)} %id_in.1, f32[1,128]{1,0:T(1,128)} %roll_in.1, f32[1,512]{1,0:T(1,128)} %old_in.1, f32[1,512]{1,0:T(1,128)} %adv_in.1, ...), custom_call_target="tpu_custom_call" | custom-call | tf_op jit(solution)/shard_map/pallas_call | solution.py:423
  110.2 1.4 %fusion = (f32[1,512]{1,0:T(1,128)}, f32[1,512]{1,0:T(1,128)}) fusion(f32[8,512]{1,0:T(8,128)} %shard_map.112), kind=kLoop, calls=%fused_computation.1 | loop fusion | bytes 8192 | tf_op jit(solution)/shard_map/slice | solution.py:453
  111.6 1.3 %slice_reduce_fusion = f32[3]{0:T(128)} fusion(f32[8,512]{1,0:T(8,128)} %shard_map.112), kind=kLoop, calls=%fused_computation | loop fusion | bytes 24 | tf_op jit(solution)/shard_map/slice | solution.py:453
where the time goes:
time: 113 us
  Pallas kernels  107 us (95%)
  local copies, waits for them, and re-layouts  3.95 us (3%)
  between operations  1.94 us (2%)
    pallas_call x1, Pallas kernels, shards(): pl.pallas_call(functools.partial(kernel, c), out_shape=jax.ShapeDtypeStru...  107 us
    slice x2, local copies, waits for them, and re-layouts, shards(): return (out[0:1], out[1:2], out[2:5, 0])  2.69 us

commit v1 on v0

v1 whole, which is shorter than its diff:
```python
import functools

import jax
import jax.numpy as jnp
from jax import lax
from jax.experimental import pallas as pl
from jax.experimental.pallas import tpu as pltpu
from jax.sharding import PartitionSpec as P

MESH = pl.DeviceIdType.MESH
clip_eps = 0.2
kl_coef = 0.2
log_limit = 10.0
norm_eps = 1e-06
LANES = 128
LOW = -1e30
UNITS_PER_TICK = 4
LEAD = 3
Z_RING = 4
Y_RING = 8


def token_terms(new_logp, old_logp, advantages, ref_logp, live_mask, prob_square):
    shift = new_logp - old_logp
    prob_ratio = jnp.exp(jnp.clip(shift, -log_limit, log_limit))
    clipped = jnp.clip(prob_ratio, 1.0 - clip_eps, 1.0 + clip_eps)
    plain_term = prob_ratio * advantages
    bounded_term = clipped * advantages
    surrogate = jnp.minimum(plain_term, bounded_term)
    ref_gap = ref_logp - new_logp
    gap_clip = jnp.clip(ref_gap, -log_limit, log_limit)
    gap_exp = jnp.exp(gap_clip)
    kl_term = gap_exp - gap_clip - 1.0
    token_loss = live_mask * (kl_coef * kl_term - surrogate)
    gap_part = jnp.where(jnp.abs(ref_gap) < log_limit, kl_coef * (1.0 - gap_exp), 0.0)
    active = (plain_term <= bounded_term) & (jnp.abs(shift) < log_limit)
    grad_coef = live_mask * (gap_part - jnp.where(active, plain_term, 0.0))
    grad_square = grad_coef * grad_coef * (prob_square - 2.0 * jnp.exp(new_logp) + 1.0)
    return (token_loss, live_mask * kl_term, grad_square)


class Config:
    def __init__(self, mesh, tok, dz, kr, vt):
        self.dp, self.fs, self.tz = (mesh.shape[a] for a in ("dp", "fsdp", "tensor"))
        self.groups = self.fs // 2
        self.tok, self.dz, self.kr, self.vt = tok, dz, kr, vt
        self.dim = dz * self.tz
        self.resp = self.dp * self.fs
        tiles = -(-vt // LANES)
        self.half_tiles = -(-tiles // (self.groups * self.dp))
        self.half_cols = self.half_tiles * LANES
        self.block_cols = self.half_cols * self.dp
        self.steps = 16 if self.groups * self.tz <= 32 else 8
        self.rows = tok // self.steps
        self.chunks = max(j for j in range(1, self.steps + 1) if self.half_tiles % j == 0)
        self.chunk = self.half_cols // self.chunks
        self.pairs = 4
        self.per_pair = self.steps // self.pairs
        self.pair_rows = tok // self.pairs
        self.width = self.groups * self.pair_rows
        self.span = 2 if self.chunks % 2 == 0 else 1
        self.blocks = self.chunks // self.span
        self.unit_cols = self.span * self.chunk
        self.gain_rows = dz // LANES
        self.plan()

    def plan(self):
        Q, Z, J = self.steps, self.tz, self.chunks
        self.ticks = Q + Z - 1
        tau = 1.0 / (Z - 1)
        start = [0.0]
        for i in range(self.ticks - 1):
            start.append(start[-1] + tau * sum(0 <= i - s < Q for s in range(Z - 1)))

        def tick_at(t):
            return min(range(len(start)), key=lambda i: abs(start[i] - t))

        last = self.ticks - 1
        rate = 13.35 / J
        self.y_tick = [tick_at(0.85 + rate * (j + 1)) for j in range(J)]
        self.x_tick = [min(last, max(t + 1, tick_at(start[t] + 1.25))) for t in self.y_tick]
        self.r_tick = [min(last, t + 1) for t in self.x_tick]
        done, self.order, self.counts = set(), [], []
        for i in range(self.ticks + 1):
            n = 0
            for k in range(self.blocks):
                for p in range(self.pairs):
                    final = p == self.pairs - 1
                    tokens = i > last if final else (p + 1) * self.per_pair + Z - 2 <= i
                    if (p, k) in done or not tokens or self.r_tick[(k + 1) * self.span - 1] > i:
                        continue
                    if n < UNITS_PER_TICK or i >= last:
                        done.add((p, k))
                        self.order.append((p, k))
                        n += 1
            self.counts.append(len(self.order))


def lookup(index, table):
    value = jnp.int32(table[0])
    for t in range(1, len(table)):
        if table[t] != table[t - 1]:
            value = value + jnp.where(index >= t, table[t] - table[t - 1], 0)
    return value


def due(i, ticks):
    count = jnp.int32(0)
    for t in ticks:
        count = count + jnp.where(i >= t, 1, 0)
    return count


def kernel(
    c,
    hid, gain_in, w_any, id_any, roll_any, old_any, adv_any, len_in, row_in,
    out,
    id_buf, roll_buf, old_buf, adv_buf,
    x_buf, n_buf, w_stage, w_full, packs, ids_all, rel, m_buf, l_buf, q_buf, p_buf,
    row_buf, roll, s_out, s_all, t_out, t_in,
    small_sem, x_sem, stage_sem, own_sem, tok_recv, y_recv, y_send, right_send, left_send,
    wy_send, wy_recv, wx_send, wx_recv, core_send, core_recv,
    ids_send, ids_recv, pack_right, pack_left, pack_recv, roll_send, roll_recv,
    st_send, st_recv, tot_send, tot_recv,
):
    G, Z, DP, F, Q, J = c.groups, c.tz, c.dp, c.fs, c.steps, c.chunks
    x = lax.axis_index("dp")
    f = lax.axis_index("fsdp")
    z = lax.axis_index("tensor")
    g, core = f // 2, f % 2
    partner = (x, g * 2 + (1 - core), z)
    me_resp = x * F + f
    right_dev = (x, f, jnp.minimum(z + 1, Z - 1))
    left_dev = (x, f, jnp.maximum(z - 1, 0))
    has_right, has_left = z + 1 < Z, z >= 1

    def dev_g(gi):
        return (x, gi * 2 + core, z)

    def dev_x(xi):
        return (xi, f, z)

    def group(d):
        return lax.rem(g + d, G)

    def remote(src, dst, ss, rs, dev):
        return pltpu.make_async_remote_copy(
            src_ref=src, dst_ref=dst, send_sem=ss, recv_sem=rs, device_id=dev, device_id_type=MESH
        )

    def arrive(dst, rs):
        remote(dst, dst, rs, rs, partner).wait_recv()

    def begin(copy):
        copy.start()

    def sent(copy):
        copy.wait_send()

    barrier = pltpu.get_barrier_semaphore()
    peers = [dev_g(group(d)) for d in range(1, G)] + [partner]
    peers += [dev_x(lax.rem(x + d, DP)) for d in range(1, DP)]
    for dev in peers:
        pl.semaphore_signal(barrier, inc=1, device_id=dev, device_id_type=MESH)
    for cond, dev in ((has_right, right_dev), (has_left, left_dev)):
        @pl.when(cond)
        def _(dev=dev):
            pl.semaphore_signal(barrier, inc=1, device_id=dev, device_id_type=MESH)

    zcols = pl.ds(pl.multiple_of(z * c.dz, c.dz), c.dz)
    fcols = pl.ds(pl.multiple_of(f * c.kr, c.kr), c.kr)
    load_x = pltpu.make_async_copy(hid, x_buf.at[g, :, zcols], x_sem)
    load_x.start()
    smalls = [
        pltpu.make_async_copy(a, b, small_sem.at[n])
        for n, (a, b) in enumerate(
            ((id_any, id_buf), (roll_any, roll_buf), (old_any, old_buf), (adv_any, adv_buf))
        )
    ]
    for copy in smalls:
        copy.start()

    def weight_loads(act):
        for own in (False, True):
            for gi in range(G):
                for h in range(DP):
                    start = gi * c.block_cols + h * c.half_cols
                    size = max(0, min(c.half_cols, c.vt - start))
                    src = w_any.at[pl.ds(start, size), :]

                    @pl.when(gi == g if own else (gi != g) & (x == h))
                    def _():
                        if own:
                            dst, sem = w_full.at[pl.ds(h * c.half_cols, size), fcols], own_sem.at[h]
                        else:
                            dst, sem = w_stage.at[gi, pl.ds(0, size), :], stage_sem.at[gi]
                        act(own, size, lambda: pltpu.make_async_copy(src, dst, sem), gi, h)

    def load_begin(own, size, copy, gi, h):
        if size:
            copy().start()
        if size < c.half_cols:
            zeros = jnp.zeros((c.half_cols - size, c.kr), w_full.dtype)
            if own:
                w_full[pl.ds(h * c.half_cols + size, c.half_cols - size), fcols] = zeros
            else:
                w_stage[gi, size:, :] = zeros

    weight_loads(load_begin)

    gain = gain_in[...].astype(jnp.float32).reshape(1, c.dz)
    for r in range(c.gain_rows):
        packs[z, r : r + 1, :] = gain[:, r * LANES : (r + 1) * LANES]
    part = roll_buf.shape[1]
    smalls[1].wait()
    tail = [roll_buf[...]] if part == LANES else [roll_buf[...], jnp.zeros((1, LANES - part), jnp.float32)]
    packs[z, c.gain_rows :, :] = jnp.broadcast_to(
        jnp.concatenate(tail, axis=1), (8 - c.gain_rows, LANES)
    )
    m_buf[...] = jnp.full(m_buf.shape, LOW, jnp.float32)
    for ref in (l_buf, q_buf, p_buf):
        ref[...] = jnp.zeros(ref.shape, jnp.float32)
    smalls[0].wait()
    ids_all[g] = id_buf[...]
    load_x.wait()

    neighbours = jnp.where(has_right, 1, 0) + jnp.where(has_left, 1, 0)
    pl.semaphore_wait(barrier, len(peers) + neighbours)

    def piece(gi, q, zi):
        return x_buf.at[
            gi, pl.ds(pl.multiple_of(q * c.rows, c.rows), c.rows), pl.ds(pl.multiple_of(zi * c.dz, c.dz), c.dz)
        ]

    def w_block(fi, h, j):
        return w_full.at[
            pl.ds(pl.multiple_of(h * c.half_cols + j * c.chunk, c.chunk), c.chunk),
            pl.ds(pl.multiple_of(fi * c.kr, c.kr), c.kr),
        ]

    def y_tokens(q, act):
        for d in range(1, G):
            act(remote(piece(g, q, z), piece(g, q, z), y_send.at[d - 1], y_recv.at[G - d - 1, lax.rem(q, Y_RING)], dev_g(group(d))))

    def y_weights(j, act):
        for d in range(1, G):
            gi = group(d)
            src = w_stage.at[gi, pl.ds(pl.multiple_of(j * c.chunk, c.chunk), c.chunk), :]
            act(remote(src, w_block(f, x, j), wy_send.at[d - 1], wy_recv.at[G - d - 1, j], dev_g(gi)))

    def hop_ends(s):
        return ((z - s >= 0, jnp.maximum(z - s, 0), has_right, right_dev, right_send, pack_right),
                (z + s < Z, jnp.minimum(z + s, Z - 1), has_left, left_dev, left_send, pack_left))

    def hop_wait(q, s, d):
        gi = group(d)
        if s == 0:
            arrive(piece(gi, q, z), y_recv.at[d - 1, lax.rem(q, Y_RING)])
            return
        for ok, zi, _, _, _, _ in hop_ends(s):
            @pl.when(ok)
            def _():
                arrive(piece(gi, q, zi), tok_recv.at[gi, lax.rem(q, Z_RING), zi])

    def hop_send(q, s, gi, act):
        for ok, zi, has, dev, sem, _ in hop_ends(s):
            @pl.when(ok & has)
            def _():
                act(remote(piece(gi, q, zi), piece(gi, q, zi), sem.at[gi, zi], tok_recv.at[gi, lax.rem(q, Z_RING), zi], dev))

    def pack_wait(s):
        for ok, zi, _, _, _, _ in hop_ends(s):
            @pl.when(ok)
            def _():
                arrive(packs.at[zi], pack_recv.at[zi])

    def pack_hop(s, act):
        for ok, zi, has, dev, _, sem in hop_ends(s):
            @pl.when(ok & has)
            def _():
                act(remote(packs.at[zi], packs.at[zi], sem.at[zi], pack_recv.at[zi], dev))

    def core_pass(src, fi, h, j, act):
        gi = fi // 2
        act(remote(src, w_block(fi, h, j), core_send.at[gi, h], core_recv.at[j], partner))

    def x_weights(d, fi, j, act):
        for dx in range(1, DP):
            act(remote(w_block(fi, x, j), w_block(fi, x, j), wx_send.at[d - 1, dx - 1],
                       wx_recv.at[d - 1, DP - dx - 1, j], dev_x(lax.rem(x + dx, DP))))

    def ids_move(act):
        for d in range(1, G):
            act(remote(id_buf, ids_all.at[g], ids_send.at[d - 1], ids_recv.at[G - d - 1], dev_g(group(d))))

    def roll_move(act):
        for dx in range(DP):
            for df in range(F):
                if dx or df:
                    act(remote(row_buf, roll.at[me_resp], roll_send, roll_recv,
                               (lax.rem(x + dx, DP), lax.rem(f + df, F), z)))

    def stats_move(p, late, act):
        for s in range(Z - 1, -1, -1):
            for d in range(G):
                if s or d:
                    gi, zi = group(d), lax.rem(z + s, Z)
                    act(remote(s_out.at[p, gi], s_all.at[p * (G * Z) + g * Z + z], st_send.at[late], st_recv.at[late],
                               (x, gi * 2 + core, zi)))

    def normalize(q):
        rows = pl.ds(pl.multiple_of(q * c.rows, c.rows), c.rows)
        for gi in range(G):
            values = x_buf[gi, rows, :].astype(jnp.float32)
            inv = lax.rsqrt(jnp.sum(values * values, axis=1, keepdims=True) / c.dim + norm_eps)
            to = (q // c.per_pair) * c.width + gi * c.pair_rows + (q % c.per_pair) * c.rows
            there = pl.ds(pl.multiple_of(to, c.rows), c.rows)
            for zi in range(Z):
                for r in range(c.gain_rows):
                    here = slice(zi * c.dz + r * LANES, zi * c.dz + (r + 1) * LANES)
                    scaled = values[:, here] * inv * packs[zi, r : r + 1, :]
                    n_buf[there, here] = scaled.astype(jnp.bfloat16)

    def unit(p, k):
        tokens = n_buf[pl.ds(pl.multiple_of(p * c.width, c.width), c.width), :]
        index = lax.broadcasted_iota(jnp.int32, (c.unit_cols // 8, 8, 1), 0) * 8 + lax.broadcasted_iota(
            jnp.int32, (c.unit_cols // 8, 8, 1), 1
        )
        for h in range(DP):
            off = h * c.half_cols + k * c.unit_cols
            cols = pl.ds(pl.multiple_of(off, c.chunk), c.unit_cols)
            logits = lax.dot_general(
                w_full[cols, :], tokens, (((1,), (1,)), ((), ())), preferred_element_type=jnp.float32
            ).reshape(c.unit_cols // 8, 8, c.width)
            valid = c.vt - g * c.block_cols - off
            place = rel[p] - off
            p_buf[p] = p_buf[p] + jnp.sum(jnp.where(index == place[None], logits, 0.0), axis=0)
            logits = jnp.where(index < valid, logits, LOW)
            before = m_buf[p]
            top = jnp.maximum(before, jnp.max(logits, axis=0))
            scale = jnp.exp(before - top)
            e = jnp.exp(logits - top[None])
            m_buf[p] = top
            l_buf[p] = l_buf[p] * scale + jnp.sum(e, axis=0)
            q_buf[p] = q_buf[p] * (scale * scale) + jnp.sum(e * e, axis=0)

    def collect(p):
        m_p = m_buf[p]
        top = jnp.max(m_p, axis=0, keepdims=True)
        scale = jnp.exp(m_p - top)
        total = jnp.sum(l_buf[p] * scale, axis=0, keepdims=True)
        square = jnp.sum(q_buf[p] * (scale * scale), axis=0, keepdims=True)
        picked = jnp.sum(p_buf[p], axis=0, keepdims=True)
        values = jnp.concatenate([top, total, square, picked, jnp.zeros((4, c.width), jnp.float32)], axis=0)
        for gi in range(G):
            s_out[p, gi] = values[:, gi * c.pair_rows : (gi + 1) * c.pair_rows]

    def collect_send(p, late):
        collect(p)
        stats_move(p, late, begin)
        s_all[p * (G * Z) + g * Z + z] = s_out[p, g]

    pack_hop(0, begin)
    for q in range(min(2, Q)):
        y_tokens(q, begin)
    ids_move(begin)

    def wait_loads(stage):
        def act(own, size, copy, gi, h):
            if size and own != stage:
                copy().wait()
        weight_loads(act)

    def tick(i, seen):
        y_first, x_first, r_first, u_first = seen
        @pl.when(i == 0)
        def _():
            wait_loads(True)
            for q in range(2, LEAD):
                y_tokens(q, begin)
            for j in range(min(LEAD - 1, J)):
                y_weights(j, begin)

        @pl.when(i + LEAD < Q)
        def _():
            y_tokens(i + LEAD, begin)

        @pl.when(i + LEAD - 1 < J)
        def _():
            y_weights(i + LEAD - 1, begin)

        for s in range(Z):
            q = i - s

            @pl.when((q >= 0) & (q < Q))
            def _(s=s, q=q):
                if s:
                    @pl.when(q == 0)
                    def _():
                        pack_wait(s)
                        if s < Z - 1:
                            pack_hop(s, begin)
                for d in range(G):
                    if s or d:
                        hop_wait(q, s, d)
                    if s < Z - 1:
                        hop_send(q, s, group(d), begin)

        @pl.when(i == 1)
        def _():
            wait_loads(False)

        @pl.when((i >= 1) & (i - 1 < J))
        def _():
            for h in range(DP):
                core_pass(w_block(f, h, i - 1), f, h, i - 1, begin)

        y_end = due(i, c.y_tick)

        @pl.loop(y_first, y_end)
        def _(j):
            for d in range(1, G):
                gi = group(d)
                fi = gi * 2 + core
                arrive(w_block(fi, x, j), wy_recv.at[d - 1, j])
                x_weights(d, fi, j, begin)
                core_pass(w_block(fi, x, j), fi, x, j, begin)

        x_end = due(i, c.x_tick)

        @pl.loop(x_first, x_end)
        def _(j):
            for d in range(1, G):
                gi = group(d)
                fi = gi * 2 + core
                for dx in range(1, DP):
                    xi = lax.rem(x + dx, DP)
                    arrive(w_block(fi, xi, j), wx_recv.at[d - 1, dx - 1, j])
                    core_pass(w_block(fi, xi, j), fi, xi, j, begin)

        q = i - (Z - 1)

        @pl.when((q >= 0) & (q < Q))
        def _():
            normalize(q)

        @pl.when(i == Z)
        def _():
            for zi in range(Z):
                row_buf[:, zi * part : (zi + 1) * part] = packs[zi, c.gain_rows : c.gain_rows + 1, :part]
            for d in range(1, G):
                arrive(ids_all.at[group(d)], ids_recv.at[d - 1])
            base = z * c.vt + g * c.block_cols
            for p in range(c.pairs):
                for gi in range(G):
                    ids = ids_all[gi, :, p * c.pair_rows : (p + 1) * c.pair_rows]
                    rel[p, :, gi * c.pair_rows : (gi + 1) * c.pair_rows] = jnp.broadcast_to(
                        ids - base, (8, c.pair_rows)
                    )

        r_end = due(i, c.r_tick)

        @pl.loop(r_first, r_end)
        def _(j):
            arrive(w_full.at[pl.ds(0, G * DP * c.kr * c.chunk // c.dim), :], core_recv.at[j])

        @pl.when(i == c.ticks)
        def _():
            roll_move(begin)
            pl.loop(0, c.pairs - 1)(lambda p: collect_send(p, 0))

        u_end = lookup(i, c.counts)

        @pl.loop(u_first, u_end)
        def _(u):
            unit(lookup(u, [p for p, _ in c.order]), lookup(u, [k for _, k in c.order]))

        return y_end, x_end, r_end, u_end

    lax.fori_loop(0, c.ticks + 1, tick, (jnp.int32(0),) * 4)
    collect_send(c.pairs - 1, 1)

    for copy in smalls[2:]:
        copy.wait()
    def done(ref, sem):
        remote(ref, ref, sem, sem, partner).wait_send()

    def features(gi, zi):
        return x_buf.at[gi, :, pl.ds(pl.multiple_of(zi * c.dz, c.dz), c.dz)]

    stage = w_stage.at[0]
    for d in range(1, G):
        done(features(g, z), y_send.at[d - 1])
        done(stage, wy_send.at[d - 1])
        for dx in range(1, DP):
            done(stage, wx_send.at[d - 1, dx - 1])
    for gi in range(G):
        for h in range(DP):
            done(stage, core_send.at[gi, h])
        for zi in range(Z):
            for cond, sem in (((zi <= z) & has_right, right_send), ((zi >= z) & has_left, left_send)):
                @pl.when(cond)
                def _():
                    done(features(gi, zi), sem.at[gi, zi])

    for s in range(Z - 1):
        pack_hop(s, sent)
    ids_move(sent)
    roll[me_resp] = row_buf[...]
    arrive(roll.at[pl.ds(0, c.resp - 1)], roll_recv)
    ref = jnp.zeros((1, c.tok), jnp.float32)
    row = row_in[...]
    for r in range(c.resp):
        ref = ref + jnp.where(row == r, roll[r], 0.0)
    position = lax.broadcasted_iota(jnp.int32, (1, c.tok), 1)
    live = jnp.where(position < len_in[...], 1.0, 0.0)
    old, adv = old_buf[...], adv_buf[...]

    tiles = G * Z - 1
    arrive(s_all.at[pl.ds(0, (c.pairs - 1) * tiles)], st_recv.at[0])
    arrive(s_all.at[pl.ds(0, tiles)], st_recv.at[1])
    every = [(gi, zi) for gi in range(G) for zi in range(Z)]

    def stat(gi, zi, k):
        return jnp.concatenate([s_all[p * (G * Z) + gi * Z + zi, k : k + 1, :] for p in range(c.pairs)], axis=1)

    top = stat(0, 0, 0)
    for gi, zi in every[1:]:
        top = jnp.maximum(top, stat(gi, zi, 0))
    total = square = picked = jnp.zeros((1, c.tok), jnp.float32)
    for gi, zi in every:
        scale = jnp.exp(stat(gi, zi, 0) - top)
        total = total + stat(gi, zi, 1) * scale
        square = square + stat(gi, zi, 2) * (scale * scale)
        picked = picked + stat(gi, zi, 3)
    new_logp = picked - top - jnp.log(total)
    prob_square = square / (total * total)
    token_loss, kl_part, grad_part = token_terms(new_logp, old, adv, ref, live, prob_square)
    sums = [jnp.sum(v, axis=1, keepdims=True) for v in (live, token_loss, kl_part, grad_part)]
    t_out[...] = jnp.concatenate(
        [jnp.broadcast_to(v, (1, LANES)) for v in sums] + [jnp.zeros((4, LANES), jnp.float32)], axis=0
    )

    def totals_move(act):
        for dx in range(DP):
            for df in range(F):
                if dx or df:
                    act(remote(t_out, t_in.at[me_resp], tot_send, tot_recv,
                               (lax.rem(x + dx, DP), lax.rem(f + df, F), z)))

    totals_move(begin)
    t_in[me_resp] = t_out[...]
    out[0:1, :] = new_logp
    out[1:2, :] = token_loss
    out[3:8, :] = jnp.zeros((5, c.tok), jnp.float32)
    done(roll.at[pl.ds(0, c.resp - 1)], roll_send)
    done(s_all.at[pl.ds(0, (c.pairs - 1) * tiles)], st_send.at[0])
    done(s_all.at[pl.ds(0, tiles)], st_send.at[1])
    arrive(t_in.at[pl.ds(0, c.resp - 1)], tot_recv)
    totals = sum(t_in[r] for r in range(c.resp))
    count = totals[0:1]
    lane = lax.broadcasted_iota(jnp.int32, (1, LANES), 1)
    means = jnp.where(lane == 0, totals[1:2] / count,
                      jnp.where(lane == 1, totals[2:3] / count, jnp.sqrt(totals[3:4] / count)))
    out[2:3, :] = jnp.concatenate([means] * (c.tok // LANES), axis=1)
    done(t_in.at[pl.ds(0, c.resp - 1)], tot_send)


def split(src, logp, loss, summary):
    logp[...] = src[0:1, :]
    loss[...] = src[1:2, :]
    summary[...] = src[2:3, 0:3].reshape(3)


def shards(c_of, hidden, norm_gain, head_weight, token_ids, lengths, old_logp, advantages, rollout_logp, rollout_row):
    c = c_of(hidden.shape[0], hidden.shape[1], head_weight.shape[0], head_weight.shape[1])
    G, Z, DP, F, Q, J = c.groups, c.tz, c.dp, c.fs, c.steps, c.chunks
    vmem = pl.BlockSpec(memory_space=pltpu.VMEM)
    hbm = pl.BlockSpec(memory_space=pl.ANY)
    dma = lambda *shape: pltpu.SemaphoreType.DMA(shape)
    one_sem = pltpu.SemaphoreType.DMA
    f32, i32, b16 = jnp.float32, jnp.int32, jnp.bfloat16
    one = lambda dtype, lead=(): pltpu.VMEM((*lead, 1, c.tok), dtype)
    lanes = lambda dtype: pltpu.VMEM((c.pairs, 8, c.width), dtype)
    out = pl.pallas_call(
        functools.partial(kernel, c),
        out_shape=jax.ShapeDtypeStruct((8, c.tok), f32),
        in_specs=[hbm, vmem, hbm, hbm, hbm, hbm, hbm, vmem, vmem],
        out_specs=vmem,
        scratch_shapes=[
            one(i32), pltpu.VMEM(rollout_logp.shape, f32), one(f32), one(f32),
            pltpu.VMEM((G, c.tok, c.dim), b16),
            pltpu.VMEM((c.pairs * c.width, c.dim), b16),
            pltpu.VMEM((G, c.half_cols, c.kr), b16),
            pltpu.VMEM((c.block_cols, c.dim), b16),
            pltpu.VMEM((Z, 8, LANES), f32),
            one(i32, (G,)),
            lanes(i32), lanes(f32), lanes(f32), lanes(f32), lanes(f32),
            one(f32), one(f32, (c.resp,)),
            pltpu.VMEM((c.pairs, G, 8, c.pair_rows), f32),
            pltpu.VMEM((c.pairs * G * Z, 8, c.pair_rows), f32),
            pltpu.VMEM((8, LANES), f32),
            pltpu.VMEM((c.resp, 8, LANES), f32),
            dma(4), one_sem, dma(G), dma(DP), dma(G, Z_RING, Z), dma(G - 1, Y_RING), dma(G - 1), dma(G, Z), dma(G, Z),
            dma(G - 1), dma(G - 1, J), dma(G - 1, DP - 1), dma(G - 1, DP - 1, J), dma(G, DP), dma(J),
            dma(G - 1), dma(G - 1), dma(Z), dma(Z), dma(Z), one_sem, one_sem,
            dma(2), dma(2), one_sem, one_sem,
        ],
        compiler_params=pltpu.CompilerParams(
            collective_id=0, has_side_effects=True, vmem_limit_bytes=64 * 1024 * 1024 - 65536
        ),
    )(hidden, norm_gain, head_weight.T, token_ids, rollout_logp, old_logp, advantages,
      lengths.reshape(1, 1), rollout_row.reshape(1, 1))
    row = lambda n: jax.ShapeDtypeStruct((1, c.tok), f32)
    return pl.pallas_call(
        split,
        out_shape=(row(0), row(1), jax.ShapeDtypeStruct((3,), f32)),
        in_specs=[vmem],
        out_specs=(vmem, vmem, vmem),
    )(out)


def solution(mesh):
    rows = ("dp", "fsdp")
    in_specs = (
        P(rows, "tensor"), P("tensor"), P("fsdp", "tensor"), P(rows, None), P(rows),
        P(rows, None), P(rows, None), P(rows, "tensor"), P(rows),
    )
    out_specs = (P(rows, None), P(rows, None), P())
    return jax.shard_map(
        functools.partial(shards, functools.partial(Config, mesh)),
        mesh=mesh, in_specs=in_specs, out_specs=out_specs, check_vma=False,
    )
```

time: 113 us -> 105 us (0.929)
  Pallas kernels: 107 us -> 103 us
  local copies, waits for them, and re-layouts: 3.95 us -> 0 us
    pallas_call x1, Pallas kernels: 107 us -> 102 us  [shards(): pl.pallas_call(functools.partial(kernel, c), out_shape=jax.ShapeDtypeStru...]
    slice x2 -> x0, local copies, waits for them, and re-layouts: 2.69 us -> none  [shards(): return (out[0:1], out[1:2], out[2:5, 0])]
    pallas_call x0 -> x1, Pallas kernels: none -> 1.3 us  [shards(): pl.pallas_call(split, out_shape=(row(0), row(1), jax.ShapeDtypeStruct((3,...]
    broadcast_in_dim x1 -> x0, local copies, waits for them, and re-layouts: 1.26 us -> none  [shards(): norm_gain[None, :]]
where the time goes in v1:
time: 105 us
  Pallas kernels  103 us (98%)
  between operations  1.93 us (2%)
    pallas_call x1, Pallas kernels, shards(): pl.pallas_call(functools.partial(kernel, c), out_shape=jax.ShapeDtypeStru...  102 us

profile of v1, /device:TPU:0, one launch (start us, length us, event | category | flops | bytes accessed | tf_op | source)
XLA Modules:
  0.0 104.9 jit_solution(41559317313791497)
XLA Ops:
  1.9 101.7 %shard_map.112.src = f32[8,512]{1,0:T(8,128)} custom-call(bf16[512,512]{1,0:T(8,128)(2,1)} %hid.1, bf16[512]{0:T(512)(128)(2,1)} %gain_in.1, bf16[8032,512]{1,0:T(8,128)(2,1)} %bitcast.5, s32[1,512]{1,0:T(1,128)} %id_any.1, f32[1,128]{1,0:T(1,128)} %roll_any.1, f32[1,512]{1,0:T(1,128)} %old_any.1, f32[1,512]{1,0:T(1,128)} %adv_any.1, s32[1,1]{1,0:T(1,128)} %bitcast.3.len_in, ...), custom_call_target="tpu_custom_call" | custom-call | tf_op jit(solution)/shard_map/pallas_call | solution.py:585
  103.6 1.3 %shard_map.113 = (f32[1,512]{1,0:T(1,128)}, f32[1,512]{1,0:T(1,128)}, f32[3]{0:T(128)}) custom-call(f32[8,512]{1,0:T(8,128)} %shard_map.112.src), custom_call_target="tpu_custom_call" | custom-call | tf_op jit(solution)/shard_map/pallas_call | solution.py:615

commit v2 on v1

--- a/solution.py
+++ b/solution.py
@@ -14,10 +14,10 @@
 norm_eps = 1e-06
 LANES = 128
 LOW = -1e30
-UNITS_PER_TICK = 4
+UNITS_PER_TICK = 2
 LEAD = 3
 Z_RING = 4
-Y_RING = 8
+TICK, W_STEP, W_AHEAD, Y_LAG, X_LAG, SLACK = 4.25, 2.8, 3, 3.2, 2.4, 1.0
 
 
 def token_terms(new_logp, old_logp, advantages, ref_logp, live_mask, prob_square):
@@ -50,44 +50,52 @@
         self.half_tiles = -(-tiles // (self.groups * self.dp))
         self.half_cols = self.half_tiles * LANES
         self.block_cols = self.half_cols * self.dp
-        self.steps = 16 if self.groups * self.tz <= 32 else 8
-        self.rows = tok // self.steps
-        self.chunks = max(j for j in range(1, self.steps + 1) if self.half_tiles % j == 0)
+        self.rows = 64
+        self.group_steps = tok // self.rows
+        self.steps = self.groups * self.group_steps
+        self.chunks = max(j for j in range(1, 17) if self.half_tiles % j == 0)
         self.chunk = self.half_cols // self.chunks
-        self.pairs = 4
-        self.per_pair = self.steps // self.pairs
-        self.pair_rows = tok // self.pairs
-        self.width = self.groups * self.pair_rows
-        self.span = 2 if self.chunks % 2 == 0 else 1
+        self.width = 256
+        self.per_pair = self.width // self.rows
+        self.group_pairs = tok // self.width
+        self.pairs = self.groups * self.group_pairs
+        self.span = next(n for n in (4, 2, 1) if self.chunks % n == 0)
         self.blocks = self.chunks // self.span
         self.unit_cols = self.span * self.chunk
         self.gain_rows = dz // LANES
         self.plan()
 
     def plan(self):
-        Q, Z, J = self.steps, self.tz, self.chunks
-        self.ticks = Q + Z - 1
-        tau = 1.0 / (Z - 1)
-        start = [0.0]
-        for i in range(self.ticks - 1):
-            start.append(start[-1] + tau * sum(0 <= i - s < Q for s in range(Z - 1)))
-
-        def tick_at(t):
-            return min(range(len(start)), key=lambda i: abs(start[i] - t))
-
+        N, Z, J, T = self.steps, self.tz, self.chunks, self.group_steps
+        self.ticks = N + Z - 1
         last = self.ticks - 1
-        rate = 13.35 / J
-        self.y_tick = [tick_at(0.85 + rate * (j + 1)) for j in range(J)]
-        self.x_tick = [min(last, max(t + 1, tick_at(start[t] + 1.25))) for t in self.y_tick]
-        self.r_tick = [min(last, t + 1) for t in self.x_tick]
+        at = [TICK * (n - 0.3) if n < N + 1 else TICK * (N + 0.7) + (n - N - 1) * TICK / 2 for n in range(self.ticks)]
+
+        def tick_at(t, low):
+            return min([n for n in range(low, last) if at[n] >= t - SLACK], default=last)
+
+        alone = max(0, T - LEAD)
+        step = W_STEP * N / J
+        self.w_tick, self.y_tick, self.x_tick, self.r_tick = [], [], [], []
+        x_free = 0.0
+        for j in range(J):
+            early = W_AHEAD + TICK / step * alone
+            n = max(0, -(-(j + 1 - W_AHEAD) * step // TICK)) if j < early else alone + (j + 1 - early) * N / J
+            self.w_tick.append(min(last, int(n)))
+            t = Y_LAG + step * (j + 1) + (max(0, j + 1 - early + W_AHEAD) * (TICK - step) if j + 1 > early - W_AHEAD else 0)
+            y = tick_at(t, self.w_tick[-1] + 1)
+            x_free = max(x_free, at[y]) + step
+            x = tick_at(x_free + X_LAG, y + 1)
+            r = min(last, x + 1)
+            self.y_tick.append(y)
+            self.x_tick.append(x)
+            self.r_tick.append(r)
         done, self.order, self.counts = set(), [], []
-        for i in range(self.ticks + 1):
+        for i in range(self.ticks):
             n = 0
             for k in range(self.blocks):
-                for p in range(self.pairs):
-                    final = p == self.pairs - 1
-                    tokens = i > last if final else (p + 1) * self.per_pair + Z - 2 <= i
-                    if (p, k) in done or not tokens or self.r_tick[(k + 1) * self.span - 1] > i:
+                for p in range(self.pairs - 1):
+                    if (p, k) in done or (p + 1) * self.per_pair + Z - 2 > i or self.r_tick[(k + 1) * self.span - 1] > i:
                         continue
                     if n < UNITS_PER_TICK or i >= last:
                         done.add((p, k))
@@ -123,7 +131,7 @@
     ids_send, ids_recv, pack_right, pack_left, pack_recv, roll_send, roll_recv,
     st_send, st_recv, tot_send, tot_recv,
 ):
-    G, Z, DP, F, Q, J = c.groups, c.tz, c.dp, c.fs, c.steps, c.chunks
+    G, Z, DP, F, N, T, J = c.groups, c.tz, c.dp, c.fs, c.steps, c.group_steps, c.chunks
     x = lax.axis_index("dp")
     f = lax.axis_index("fsdp")
     z = lax.axis_index("tensor")
@@ -238,9 +246,13 @@
             pl.ds(pl.multiple_of(fi * c.kr, c.kr), c.kr),
         ]
 
-    def y_tokens(q, act):
+    def y_tokens(n, act):
         for d in range(1, G):
-            act(remote(piece(g, q, z), piece(g, q, z), y_send.at[d - 1], y_recv.at[G - d - 1, lax.rem(q, Y_RING)], dev_g(group(d))))
+            q = n - (G - d) * T
+
+            @pl.when((q >= 0) & (q < T))
+            def _(d=d, q=q):
+                act(remote(piece(g, q, z), piece(g, q, z), y_send.at[d - 1], y_recv.at[G - d - 1, q], dev_g(group(d))))
 
     def y_weights(j, act):
         for d in range(1, G):
@@ -252,21 +264,27 @@
         return ((z - s >= 0, jnp.maximum(z - s, 0), has_right, right_dev, right_send, pack_right),
                 (z + s < Z, jnp.minimum(z + s, Z - 1), has_left, left_dev, left_send, pack_left))
 
-    def hop_wait(q, s, d):
-        gi = group(d)
+    def locate(n):
+        return group(n // T), lax.rem(n, T), lax.rem(n, Z_RING)
+
+    def hop_wait(n, s):
+        gi, q, slot = locate(n)
         if s == 0:
-            arrive(piece(gi, q, z), y_recv.at[d - 1, lax.rem(q, Y_RING)])
+            @pl.when(n >= T)
+            def _():
+                arrive(piece(gi, q, z), y_recv.at[n // T - 1, q])
             return
         for ok, zi, _, _, _, _ in hop_ends(s):
             @pl.when(ok)
             def _():
-                arrive(piece(gi, q, zi), tok_recv.at[gi, lax.rem(q, Z_RING), zi])
-
-    def hop_send(q, s, gi, act):
+                arrive(piece(gi, q, zi), tok_recv.at[slot, zi])
+
+    def hop_send(n, s, act):
+        gi, q, slot = locate(n)
         for ok, zi, has, dev, sem, _ in hop_ends(s):
             @pl.when(ok & has)
             def _():
-                act(remote(piece(gi, q, zi), piece(gi, q, zi), sem.at[gi, zi], tok_recv.at[gi, lax.rem(q, Z_RING), zi], dev))
+                act(remote(piece(gi, q, zi), piece(gi, q, zi), sem.at[zi], tok_recv.at[slot, zi], dev))
 
     def pack_wait(s):
         for ok, zi, _, _, _, _ in hop_ends(s):
@@ -301,25 +319,27 @@
                                (lax.rem(x + dx, DP), lax.rem(f + df, F), z)))
 
     def stats_move(p, late, act):
+        d, half = p // c.group_pairs, lax.rem(p, c.group_pairs)
+        gi = group(d)
         for s in range(Z - 1, -1, -1):
-            for d in range(G):
-                if s or d:
-                    gi, zi = group(d), lax.rem(z + s, Z)
-                    act(remote(s_out.at[p, gi], s_all.at[p * (G * Z) + g * Z + z], st_send.at[late], st_recv.at[late],
-                               (x, gi * 2 + core, zi)))
-
-    def normalize(q):
-        rows = pl.ds(pl.multiple_of(q * c.rows, c.rows), c.rows)
-        for gi in range(G):
-            values = x_buf[gi, rows, :].astype(jnp.float32)
-            inv = lax.rsqrt(jnp.sum(values * values, axis=1, keepdims=True) / c.dim + norm_eps)
-            to = (q // c.per_pair) * c.width + gi * c.pair_rows + (q % c.per_pair) * c.rows
-            there = pl.ds(pl.multiple_of(to, c.rows), c.rows)
-            for zi in range(Z):
-                for r in range(c.gain_rows):
-                    here = slice(zi * c.dz + r * LANES, zi * c.dz + (r + 1) * LANES)
-                    scaled = values[:, here] * inv * packs[zi, r : r + 1, :]
-                    n_buf[there, here] = scaled.astype(jnp.bfloat16)
+            def go(s=s):
+                act(remote(s_out.at[p], s_all.at[half * (G * Z) + g * Z + z], st_send.at[late], st_recv.at[late],
+                           (x, gi * 2 + core, lax.rem(z + s, Z))))
+            if s:
+                go()
+            else:
+                pl.when(d > 0)(go)
+
+    def normalize(n):
+        gi, q, _ = locate(n)
+        values = x_buf[gi, pl.ds(pl.multiple_of(q * c.rows, c.rows), c.rows), :].astype(jnp.float32)
+        inv = lax.rsqrt(jnp.sum(values * values, axis=1, keepdims=True) / c.dim + norm_eps)
+        there = pl.ds(pl.multiple_of(n * c.rows, c.rows), c.rows)
+        for zi in range(Z):
+            for r in range(c.gain_rows):
+                here = slice(zi * c.dz + r * LANES, zi * c.dz + (r + 1) * LANES)
+                scaled = values[:, here] * inv * packs[zi, r : r + 1, :]
+                n_buf[there, here] = scaled.astype(jnp.bfloat16)
 
     def unit(p, k):
         tokens = n_buf[pl.ds(pl.multiple_of(p * c.width, c.width), c.width), :]
@@ -351,18 +371,18 @@
         total = jnp.sum(l_buf[p] * scale, axis=0, keepdims=True)
         square = jnp.sum(q_buf[p] * (scale * scale), axis=0, keepdims=True)
         picked = jnp.sum(p_buf[p], axis=0, keepdims=True)
-        values = jnp.concatenate([top, total, square, picked, jnp.zeros((4, c.width), jnp.float32)], axis=0)
-        for gi in range(G):
-            s_out[p, gi] = values[:, gi * c.pair_rows : (gi + 1) * c.pair_rows]
+        s_out[p] = jnp.concatenate([top, total, square, picked, jnp.zeros((4, c.width), jnp.float32)], axis=0)
 
     def collect_send(p, late):
+        p = jnp.int32(p)
         collect(p)
         stats_move(p, late, begin)
-        s_all[p * (G * Z) + g * Z + z] = s_out[p, g]
+
+        @pl.when(p < c.group_pairs)
+        def _():
+            s_all[p * (G * Z) + g * Z + z] = s_out[p]
 
     pack_hop(0, begin)
-    for q in range(min(2, Q)):
-        y_tokens(q, begin)
     ids_move(begin)
 
     def wait_loads(stage):
@@ -372,27 +392,26 @@
         weight_loads(act)
 
     def tick(i, seen):
-        y_first, x_first, r_first, u_first = seen
+        w_first, y_first, x_first, r_first, u_first = seen
+
         @pl.when(i == 0)
         def _():
             wait_loads(True)
-            for q in range(2, LEAD):
-                y_tokens(q, begin)
-            for j in range(min(LEAD - 1, J)):
-                y_weights(j, begin)
-
-        @pl.when(i + LEAD < Q)
+
+        w_end = due(i, c.w_tick)
+
+        @pl.when(i + LEAD < N)
         def _():
             y_tokens(i + LEAD, begin)
 
-        @pl.when(i + LEAD - 1 < J)
-        def _():
-            y_weights(i + LEAD - 1, begin)
+        @pl.loop(w_first, w_end)
+        def _(j):
+            y_weights(j, begin)
 
         for s in range(Z):
             q = i - s
 
-            @pl.when((q >= 0) & (q < Q))
+            @pl.when((q >= 0) & (q < N))
             def _(s=s, q=q):
                 if s:
                     @pl.when(q == 0)
@@ -400,20 +419,21 @@
                         pack_wait(s)
                         if s < Z - 1:
                             pack_hop(s, begin)
-                for d in range(G):
-                    if s or d:
-                        hop_wait(q, s, d)
-                    if s < Z - 1:
-                        hop_send(q, s, group(d), begin)
+                hop_wait(q, s)
+                if s < Z - 1:
+                    hop_send(q, s, begin)
 
         @pl.when(i == 1)
         def _():
             wait_loads(False)
 
-        @pl.when((i >= 1) & (i - 1 < J))
-        def _():
-            for h in range(DP):
-                core_pass(w_block(f, h, i - 1), f, h, i - 1, begin)
+        for n in range(2):
+            j = 2 * (i - 1) + n
+
+            @pl.when((j >= 0) & (j < J))
+            def _(j=j):
+                for h in range(DP):
+                    core_pass(w_block(f, h, j), f, h, j, begin)
 
         y_end = due(i, c.y_tick)
 
@@ -440,7 +460,7 @@
 
         q = i - (Z - 1)
 
-        @pl.when((q >= 0) & (q < Q))
+        @pl.when((q >= 0) & (q < N))
         def _():
             normalize(q)
 
@@ -451,12 +471,10 @@
             for d in range(1, G):
                 arrive(ids_all.at[group(d)], ids_recv.at[d - 1])
             base = z * c.vt + g * c.block_cols
-            for p in range(c.pairs):
-                for gi in range(G):
-                    ids = ids_all[gi, :, p * c.pair_rows : (p + 1) * c.pair_rows]
-                    rel[p, :, gi * c.pair_rows : (gi + 1) * c.pair_rows] = jnp.broadcast_to(
-                        ids - base, (8, c.pair_rows)
-                    )
+            for d in range(G):
+                for half in range(c.group_pairs):
+                    ids = ids_all[group(d), :, half * c.width : (half + 1) * c.width]
+                    rel[d * c.group_pairs + half] = jnp.broadcast_to(ids - base, (8, c.width))
 
         r_end = due(i, c.r_tick)
 
@@ -464,20 +482,18 @@
         def _(j):
             arrive(w_full.at[pl.ds(0, G * DP * c.kr * c.chunk // c.dim), :], core_recv.at[j])
 
-        @pl.when(i == c.ticks)
-        def _():
-            roll_move(begin)
-            pl.loop(0, c.pairs - 1)(lambda p: collect_send(p, 0))
-
         u_end = lookup(i, c.counts)
 
         @pl.loop(u_first, u_end)
         def _(u):
             unit(lookup(u, [p for p, _ in c.order]), lookup(u, [k for _, k in c.order]))
 
-        return y_end, x_end, r_end, u_end
-
-    lax.fori_loop(0, c.ticks + 1, tick, (jnp.int32(0),) * 4)
+        return w_end, y_end, x_end, r_end, u_end
+
+    lax.fori_loop(0, c.ticks, tick, (jnp.int32(0),) * 5)
+    roll_move(begin)
+    pl.loop(0, c.pairs - 1)(lambda p: collect_send(p, 0))
+    pl.loop(0, c.blocks)(lambda k: unit(c.pairs - 1, k))
     collect_send(c.pairs - 1, 1)
 
     for copy in smalls[2:]:
@@ -497,11 +513,11 @@
     for gi in range(G):
         for h in range(DP):
             done(stage, core_send.at[gi, h])
-        for zi in range(Z):
-            for cond, sem in (((zi <= z) & has_right, right_send), ((zi >= z) & has_left, left_send)):
-                @pl.when(cond)
-                def _():
-                    done(features(gi, zi), sem.at[gi, zi])
+    for zi in range(Z):
+        for cond, sem in (((zi <= z) & has_right, right_send), ((zi >= z) & has_left, left_send)):
+            @pl.when(cond)
+            def _():
+                done(x_buf.at[:, :, pl.ds(zi * c.dz, c.dz)], sem.at[zi])
 
     for s in range(Z - 1):
         pack_hop(s, sent)
@@ -516,13 +532,13 @@
     live = jnp.where(position < len_in[...], 1.0, 0.0)
     old, adv = old_buf[...], adv_buf[...]
 
-    tiles = G * Z - 1
-    arrive(s_all.at[pl.ds(0, (c.pairs - 1) * tiles)], st_recv.at[0])
-    arrive(s_all.at[pl.ds(0, tiles)], st_recv.at[1])
+    early = c.group_pairs * (G * Z - 1) - Z
+    arrive(s_all.at[pl.ds(0, early)], st_recv.at[0])
+    arrive(s_all.at[pl.ds(0, Z)], st_recv.at[1])
     every = [(gi, zi) for gi in range(G) for zi in range(Z)]
 
     def stat(gi, zi, k):
-        return jnp.concatenate([s_all[p * (G * Z) + gi * Z + zi, k : k + 1, :] for p in range(c.pairs)], axis=1)
+        return jnp.concatenate([s_all[p * (G * Z) + gi * Z + zi, k : k + 1, :] for p in range(c.group_pairs)], axis=1)
 
     top = stat(0, 0, 0)
     for gi, zi in every[1:]:
@@ -554,8 +570,8 @@
     out[1:2, :] = token_loss
     out[3:8, :] = jnp.zeros((5, c.tok), jnp.float32)
     done(roll.at[pl.ds(0, c.resp - 1)], roll_send)
-    done(s_all.at[pl.ds(0, (c.pairs - 1) * tiles)], st_send.at[0])
-    done(s_all.at[pl.ds(0, tiles)], st_send.at[1])
+    done(s_all.at[pl.ds(0, early)], st_send.at[0])
+    done(s_all.at[pl.ds(0, Z)], st_send.at[1])
     arrive(t_in.at[pl.ds(0, c.resp - 1)], tot_recv)
     totals = sum(t_in[r] for r in range(c.resp))
     count = totals[0:1]
@@ -574,7 +590,7 @@
 
 def shards(c_of, hidden, norm_gain, head_weight, token_ids, lengths, old_logp, advantages, rollout_logp, rollout_row):
     c = c_of(hidden.shape[0], hidden.shape[1], head_weight.shape[0], head_weight.shape[1])
-    G, Z, DP, F, Q, J = c.groups, c.tz, c.dp, c.fs, c.steps, c.chunks
+    G, Z, DP, F, T, J = c.groups, c.tz, c.dp, c.fs, c.group_steps, c.chunks
     vmem = pl.BlockSpec(memory_space=pltpu.VMEM)
     hbm = pl.BlockSpec(memory_space=pl.ANY)
     dma = lambda *shape: pltpu.SemaphoreType.DMA(shape)
@@ -597,11 +613,11 @@
             one(i32, (G,)),
             lanes(i32), lanes(f32), lanes(f32), lanes(f32), lanes(f32),
             one(f32), one(f32, (c.resp,)),
-            pltpu.VMEM((c.pairs, G, 8, c.pair_rows), f32),
-            pltpu.VMEM((c.pairs * G * Z, 8, c.pair_rows), f32),
+            pltpu.VMEM((c.pairs, 8, c.width), f32),
+            pltpu.VMEM((c.group_pairs * G * Z, 8, c.width), f32),
             pltpu.VMEM((8, LANES), f32),
             pltpu.VMEM((c.resp, 8, LANES), f32),
-            dma(4), one_sem, dma(G), dma(DP), dma(G, Z_RING, Z), dma(G - 1, Y_RING), dma(G - 1), dma(G, Z), dma(G, Z),
+            dma(4), one_sem, dma(G), dma(DP), dma(Z_RING, Z), dma(G - 1, T), dma(G - 1), dma(Z), dma(Z),
             dma(G - 1), dma(G - 1, J), dma(G - 1, DP - 1), dma(G - 1, DP - 1, J), dma(G, DP), dma(J),
             dma(G - 1), dma(G - 1), dma(Z), dma(Z), dma(Z), one_sem, one_sem,
             dma(2), dma(2), one_sem, one_sem,

time: 105 us -> 102 us (0.971)
  Pallas kernels: 103 us -> 99.7 us
    pallas_call x1, Pallas kernels: 102 us -> 98.4 us  [shards(): pl.pallas_call(functools.partial(kernel, c), out_shape=jax.ShapeDtypeStru...]
where the time goes in v2:
time: 102 us
  Pallas kernels  99.7 us (98%)
  between operations  1.93 us (2%)
    pallas_call x1, Pallas kernels, shards(): pl.pallas_call(functools.partial(kernel, c), out_shape=jax.ShapeDtypeStru...  98.4 us

profile of v2, /device:TPU:0, one launch (start us, length us, event | category | flops | bytes accessed | tf_op | source)
XLA Modules:
  0.0 101.7 jit_solution(4490659919330106712)
XLA Ops:
  1.9 98.4 %shard_map.112.src = f32[8,512]{1,0:T(8,128)} custom-call(bf16[512,512]{1,0:T(8,128)(2,1)} %hid.1, bf16[512]{0:T(512)(128)(2,1)} %gain_in.1, bf16[8032,512]{1,0:T(8,128)(2,1)} %bitcast.5, s32[1,512]{1,0:T(1,128)} %id_any.1, f32[1,128]{1,0:T(1,128)} %roll_any.1, f32[1,512]{1,0:T(1,128)} %old_any.1, f32[1,512]{1,0:T(1,128)} %adv_any.1, s32[1,1]{1,0:T(1,128)} %bitcast.3.len_in, ...), custom_call_target="tpu_custom_call" | custom-call | tf_op jit(solution)/shard_map/pallas_call | solution.py:601
  100.3 1.3 %shard_map.113 = (f32[1,512]{1,0:T(1,128)}, f32[1,512]{1,0:T(1,128)}, f32[3]{0:T(128)}) custom-call(f32[8,512]{1,0:T(8,128)} %shard_map.112.src), custom_call_target="tpu_custom_call" | custom-call | tf_op jit(solution)/shard_map/pallas_call | solution.py:631

commit v3 on v2

--- a/solution.py
+++ b/solution.py
@@ -15,9 +15,9 @@
 LANES = 128
 LOW = -1e30
 UNITS_PER_TICK = 2
-LEAD = 3
+LEAD = 5
 Z_RING = 4
-TICK, W_STEP, W_AHEAD, Y_LAG, X_LAG, SLACK = 4.25, 2.8, 3, 3.2, 2.4, 1.0
+TICK, FILL, W_STEP, W_AHEAD, Y_HEAD, Y_LAG, X_LAG, SLACK = 4.25, 3.8, 2.8, 12.0, 7.5, 3.5, 2.4, 1.5
 
 
 def token_terms(new_logp, old_logp, advantages, ref_logp, live_mask, prob_square):
@@ -69,21 +69,21 @@
         N, Z, J, T = self.steps, self.tz, self.chunks, self.group_steps
         self.ticks = N + Z - 1
         last = self.ticks - 1
-        at = [TICK * (n - 0.3) if n < N + 1 else TICK * (N + 0.7) + (n - N - 1) * TICK / 2 for n in range(self.ticks)]
+        at = [FILL * n for n in range(Z)]
+        for n in range(Z, self.ticks):
+            at.append(at[-1] + TICK * sum(0 <= n - 1 - h < N for h in range(Z - 1)) / (Z - 1))
 
         def tick_at(t, low):
             return min([n for n in range(low, last) if at[n] >= t - SLACK], default=last)
 
-        alone = max(0, T - LEAD)
         step = W_STEP * N / J
+        alone = max(1, int((T * TICK - Y_HEAD) / step))
         self.w_tick, self.y_tick, self.x_tick, self.r_tick = [], [], [], []
         x_free = 0.0
         for j in range(J):
-            early = W_AHEAD + TICK / step * alone
-            n = max(0, -(-(j + 1 - W_AHEAD) * step // TICK)) if j < early else alone + (j + 1 - early) * N / J
-            self.w_tick.append(min(last, int(n)))
-            t = Y_LAG + step * (j + 1) + (max(0, j + 1 - early + W_AHEAD) * (TICK - step) if j + 1 > early - W_AHEAD else 0)
-            y = tick_at(t, self.w_tick[-1] + 1)
+            begin = step * j if j < alone else step * alone + (j - alone) * TICK + TICK / 3
+            self.w_tick.append(max(n for n in range(last) if n == 0 or at[n] <= begin - W_AHEAD))
+            y = tick_at(begin + step + Y_LAG, self.w_tick[-1] + 1)
             x_free = max(x_free, at[y]) + step
             x = tick_at(x_free + X_LAG, y + 1)
             r = min(last, x + 1)
@@ -121,9 +121,9 @@
 
 def kernel(
     c,
-    hid, gain_in, w_any, id_any, roll_any, old_any, adv_any, len_in, row_in,
+    hid, gain_any, w_any, id_any, roll_any, old_any, adv_any, len_any, row_any,
     out,
-    id_buf, roll_buf, old_buf, adv_buf,
+    id_buf, roll_buf, old_buf, adv_buf, gain_in, len_in, row_in,
     x_buf, n_buf, w_stage, w_full, packs, ids_all, rel, m_buf, l_buf, q_buf, p_buf,
     row_buf, roll, s_out, s_all, t_out, t_in,
     small_sem, x_sem, stage_sem, own_sem, tok_recv, y_recv, y_send, right_send, left_send,
@@ -182,7 +182,8 @@
     smalls = [
         pltpu.make_async_copy(a, b, small_sem.at[n])
         for n, (a, b) in enumerate(
-            ((id_any, id_buf), (roll_any, roll_buf), (old_any, old_buf), (adv_any, adv_buf))
+            ((id_any, id_buf), (roll_any, roll_buf), (gain_any, gain_in), (old_any, old_buf), (adv_any, adv_buf),
+             (len_any, len_in), (row_any, row_in))
         )
     ]
     for copy in smalls:
@@ -216,6 +217,7 @@
 
     weight_loads(load_begin)
 
+    smalls[2].wait()
     gain = gain_in[...].astype(jnp.float32).reshape(1, c.dz)
     for r in range(c.gain_rows):
         packs[z, r : r + 1, :] = gain[:, r * LANES : (r + 1) * LANES]
@@ -371,7 +373,7 @@
         total = jnp.sum(l_buf[p] * scale, axis=0, keepdims=True)
         square = jnp.sum(q_buf[p] * (scale * scale), axis=0, keepdims=True)
         picked = jnp.sum(p_buf[p], axis=0, keepdims=True)
-        s_out[p] = jnp.concatenate([top, total, square, picked, jnp.zeros((4, c.width), jnp.float32)], axis=0)
+        s_out[p] = jnp.concatenate([top, total, square, picked], axis=0)
 
     def collect_send(p, late):
         p = jnp.int32(p)
@@ -435,6 +437,12 @@
                 for h in range(DP):
                     core_pass(w_block(f, h, j), f, h, j, begin)
 
+        r_end = due(i, c.r_tick)
+
+        @pl.loop(r_first, r_end)
+        def _(j):
+            arrive(w_full.at[pl.ds(0, G * DP * c.kr * c.chunk // c.dim), :], core_recv.at[j])
+
         y_end = due(i, c.y_tick)
 
         @pl.loop(y_first, y_end)
@@ -476,12 +484,6 @@
                     ids = ids_all[group(d), :, half * c.width : (half + 1) * c.width]
                     rel[d * c.group_pairs + half] = jnp.broadcast_to(ids - base, (8, c.width))
 
-        r_end = due(i, c.r_tick)
-
-        @pl.loop(r_first, r_end)
-        def _(j):
-            arrive(w_full.at[pl.ds(0, G * DP * c.kr * c.chunk // c.dim), :], core_recv.at[j])
-
         u_end = lookup(i, c.counts)
 
         @pl.loop(u_first, u_end)
@@ -496,7 +498,7 @@
     pl.loop(0, c.blocks)(lambda k: unit(c.pairs - 1, k))
     collect_send(c.pairs - 1, 1)
 
-    for copy in smalls[2:]:
+    for copy in smalls[3:]:
         copy.wait()
     def done(ref, sem):
         remote(ref, ref, sem, sem, partner).wait_send()
@@ -601,10 +603,11 @@
     out = pl.pallas_call(
         functools.partial(kernel, c),
         out_shape=jax.ShapeDtypeStruct((8, c.tok), f32),
-        in_specs=[hbm, vmem, hbm, hbm, hbm, hbm, hbm, vmem, vmem],
+        in_specs=[hbm] * 9,
         out_specs=vmem,
         scratch_shapes=[
             one(i32), pltpu.VMEM(rollout_logp.shape, f32), one(f32), one(f32),
+            pltpu.VMEM(norm_gain.shape, b16), pltpu.VMEM((1, 1), i32), pltpu.VMEM((1, 1), i32),
             pltpu.VMEM((G, c.tok, c.dim), b16),
             pltpu.VMEM((c.pairs * c.width, c.dim), b16),
             pltpu.VMEM((G, c.half_cols, c.kr), b16),
@@ -613,11 +616,11 @@
             one(i32, (G,)),
             lanes(i32), lanes(f32), lanes(f32), lanes(f32), lanes(f32),
             one(f32), one(f32, (c.resp,)),
-            pltpu.VMEM((c.pairs, 8, c.width), f32),
-            pltpu.VMEM((c.group_pairs * G * Z, 8, c.width), f32),
+            pltpu.VMEM((c.pairs, 4, c.width), f32),
+            pltpu.VMEM((c.group_pairs * G * Z, 4, c.width), f32),
             pltpu.VMEM((8, LANES), f32),
             pltpu.VMEM((c.resp, 8, LANES), f32),
-            dma(4), one_sem, dma(G), dma(DP), dma(Z_RING, Z), dma(G - 1, T), dma(G - 1), dma(Z), dma(Z),
+            dma(7), one_sem, dma(G), dma(DP), dma(Z_RING, Z), dma(G - 1, T), dma(G - 1), dma(Z), dma(Z),
             dma(G - 1), dma(G - 1, J), dma(G - 1, DP - 1), dma(G - 1, DP - 1, J), dma(G, DP), dma(J),
             dma(G - 1), dma(G - 1), dma(Z), dma(Z), dma(Z), one_sem, one_sem,
             dma(2), dma(2), one_sem, one_sem,

time: 102 us -> 97.8 us (0.959)
  Pallas kernels: 99.7 us -> 95.6 us
    pallas_call x1, Pallas kernels: 98.4 us -> 94.3 us  [shards(): pl.pallas_call(functools.partial(kernel, c), out_shape=jax.ShapeDtypeStru...]
where the time goes in v3:
time: 97.8 us; the launch traced here: 97.5 us
  Pallas kernels  95.6 us (98%)
  between operations  1.93 us (2%)
    pallas_call x1, Pallas kernels, shards(): pl.pallas_call(functools.partial(kernel, c), out_shape=jax.ShapeDtypeStru...  94.3 us

profile of v3, /device:TPU:0, one launch (start us, length us, event | category | flops | bytes accessed | tf_op | source)
XLA Modules:
  0.0 97.5 jit_solution(2755056963020713713)
XLA Ops:
  1.9 94.3 %shard_map.112.src = f32[8,512]{1,0:T(8,128)} custom-call(bf16[512,512]{1,0:T(8,128)(2,1)} %hid.1, bf16[512]{0:T(512)(128)(2,1)} %gain_any.1, bf16[8032,512]{1,0:T(8,128)(2,1)} %bitcast.5, s32[1,512]{1,0:T(1,128)} %id_any.1, f32[1,128]{1,0:T(1,128)} %roll_any.1, f32[1,512]{1,0:T(1,128)} %old_any.1, f32[1,512]{1,0:T(1,128)} %adv_any.1, ...), custom_call_target="tpu_custom_call" | custom-call | tf_op jit(solution)/shard_map/pallas_call | solution.py:603
  96.2 1.3 %shard_map.113 = (f32[1,512]{1,0:T(1,128)}, f32[1,512]{1,0:T(1,128)}, f32[3]{0:T(128)}) custom-call(f32[8,512]{1,0:T(8,128)} %shard_map.112.src), custom_call_target="tpu_custom_call" | custom-call | tf_op jit(solution)/shard_map/pallas_call | solution.py:634

commit v4 on v3

--- a/solution.py
+++ b/solution.py
@@ -343,21 +343,23 @@
                 scaled = values[:, here] * inv * packs[zi, r : r + 1, :]
                 n_buf[there, here] = scaled.astype(jnp.bfloat16)
 
-    def unit(p, k):
+    def unit(p, k, halves=None, span_cols=None):
+        n_cols = span_cols or c.unit_cols
         tokens = n_buf[pl.ds(pl.multiple_of(p * c.width, c.width), c.width), :]
-        index = lax.broadcasted_iota(jnp.int32, (c.unit_cols // 8, 8, 1), 0) * 8 + lax.broadcasted_iota(
-            jnp.int32, (c.unit_cols // 8, 8, 1), 1
+        index = lax.broadcasted_iota(jnp.int32, (n_cols // 8, 8, 1), 0) * 8 + lax.broadcasted_iota(
+            jnp.int32, (n_cols // 8, 8, 1), 1
         )
-        for h in range(DP):
-            off = h * c.half_cols + k * c.unit_cols
-            cols = pl.ds(pl.multiple_of(off, c.chunk), c.unit_cols)
+        for h in (range(DP) if halves is None else halves):
+            off = h * c.half_cols + k * n_cols
+            cols = pl.ds(pl.multiple_of(off, c.chunk), n_cols)
             logits = lax.dot_general(
                 w_full[cols, :], tokens, (((1,), (1,)), ((), ())), preferred_element_type=jnp.float32
-            ).reshape(c.unit_cols // 8, 8, c.width)
+            ).reshape(n_cols // 8, 8, c.width)
             valid = c.vt - g * c.block_cols - off
             place = rel[p] - off
             p_buf[p] = p_buf[p] + jnp.sum(jnp.where(index == place[None], logits, 0.0), axis=0)
-            logits = jnp.where(index < valid, logits, LOW)
+            if (G - 1) * c.block_cols + (h + 1) * c.half_cols > c.vt:
+                logits = jnp.where(index < valid, logits, LOW)
             before = m_buf[p]
             top = jnp.maximum(before, jnp.max(logits, axis=0))
             scale = jnp.exp(before - top)
@@ -495,7 +497,12 @@
     lax.fori_loop(0, c.ticks, tick, (jnp.int32(0),) * 5)
     roll_move(begin)
     pl.loop(0, c.pairs - 1)(lambda p: collect_send(p, 0))
-    pl.loop(0, c.blocks)(lambda k: unit(c.pairs - 1, k))
+    wide = 2 if c.blocks % 2 == 0 else 1
+
+    @pl.loop(0, c.blocks // wide)
+    def _(k):
+        for h in range(DP):
+            unit(c.pairs - 1, k, (h,), wide * c.unit_cols)
     collect_send(c.pairs - 1, 1)
 
     for copy in smalls[3:]:

time: 97.8 us -> 96.9 us (level)
  no operation moved by 1% of the time
where the time goes in v4:
time: 96.9 us; the launch traced here: 96.6 us
  Pallas kernels  94.7 us (98%)
  between operations  1.93 us (2%)
    pallas_call x1, Pallas kernels, shards(): pl.pallas_call(functools.partial(kernel, c), out_shape=jax.ShapeDtypeStru...  93.4 us

profile of v4, /device:TPU:0, one launch (start us, length us, event | category | flops | bytes accessed | tf_op | source)
XLA Modules:
  0.0 96.6 jit_solution(1918423559160120283)
XLA Ops:
  1.9 93.4 %shard_map.112.src = f32[8,512]{1,0:T(8,128)} custom-call(bf16[512,512]{1,0:T(8,128)(2,1)} %hid.1, bf16[512]{0:T(512)(128)(2,1)} %gain_any.1, bf16[8032,512]{1,0:T(8,128)(2,1)} %bitcast.5, s32[1,512]{1,0:T(1,128)} %id_any.1, f32[1,128]{1,0:T(1,128)} %roll_any.1, f32[1,512]{1,0:T(1,128)} %old_any.1, f32[1,512]{1,0:T(1,128)} %adv_any.1, ...), custom_call_target="tpu_custom_call" | custom-call | tf_op jit(solution)/shard_map/pallas_call | solution.py:610
  95.3 1.3 %shard_map.113 = (f32[1,512]{1,0:T(1,128)}, f32[1,512]{1,0:T(1,128)}, f32[3]{0:T(128)}) custom-call(f32[8,512]{1,0:T(8,128)} %shard_map.112.src), custom_call_target="tpu_custom_call" | custom-call | tf_op jit(solution)/shard_map/pallas_call | solution.py:641

commit v5 on v4

--- a/solution.py
+++ b/solution.py
@@ -499,8 +499,7 @@
     pl.loop(0, c.pairs - 1)(lambda p: collect_send(p, 0))
     wide = 2 if c.blocks % 2 == 0 else 1
 
-    @pl.loop(0, c.blocks // wide)
-    def _(k):
+    for k in range(c.blocks // wide):
         for h in range(DP):
             unit(c.pairs - 1, k, (h,), wide * c.unit_cols)
     collect_send(c.pairs - 1, 1)

time: 96.9 us -> 96.6 us (level)
  no operation moved by 1% of the time
where the time goes in v5:
time: 96.6 us; the launch traced here: 96.4 us
  Pallas kernels  94.4 us (98%)
  between operations  1.93 us (2%)
    pallas_call x1, Pallas kernels, shards(): pl.pallas_call(functools.partial(kernel, c), out_shape=jax.ShapeDtypeStru...  93.1 us

profile of v5, /device:TPU:0, one launch (start us, length us, event | category | flops | bytes accessed | tf_op | source)
XLA Modules:
  0.0 96.4 jit_solution(2768120865270590965)
XLA Ops:
  1.9 93.1 %shard_map.112.src = f32[8,512]{1,0:T(8,128)} custom-call(bf16[512,512]{1,0:T(8,128)(2,1)} %hid.1, bf16[512]{0:T(512)(128)(2,1)} %gain_any.1, bf16[8032,512]{1,0:T(8,128)(2,1)} %bitcast.5, s32[1,512]{1,0:T(1,128)} %id_any.1, f32[1,128]{1,0:T(1,128)} %roll_any.1, f32[1,512]{1,0:T(1,128)} %old_any.1, f32[1,512]{1,0:T(1,128)} %adv_any.1, ...), custom_call_target="tpu_custom_call" | custom-call | tf_op jit(solution)/shard_map/pallas_call | solution.py:609
  95.1 1.3 %shard_map.113 = (f32[1,512]{1,0:T(1,128)}, f32[1,512]{1,0:T(1,128)}, f32[3]{0:T(128)}) custom-call(f32[8,512]{1,0:T(8,128)} %shard_map.112.src), custom_call_target="tpu_custom_call" | custom-call | tf_op jit(solution)/shard_map/pallas_call | solution.py:640
